TPU v7x, 32 devices: a whole 2x2x4 slice. The times are simulated.
32 devices in a mesh: rep: 2 (over y), pipe: 2 (over core), tp: 8 (over z, x).
Axes of the slice: x: 2, y: 2, z: 4, core: 2. Of those that a mesh axis runs over, the one named last changes fastest.
Arguments:
- hidden_entering: bfloat16 [2, 120, 8192], P('rep', None, 'tp'), parts along dimension 0, may hold values from -60 to 60
- segment_adapter: int32 [2, 3], P('rep'), parts along dimension 0, may hold values from 0 to 127, as said below
- segment_requests: int32 [2, 3], P('rep'), parts along dimension 0, may hold values from 10 to 40, as said below
- section_norm_gain: float32 [2, 8192], P('pipe'), may hold values from 0.25 to 1.75
- up_matrix: bfloat16 [2, 14336, 8192], P('pipe', 'tp'), may hold values from -0.0625 to 0.0625
- down_matrix: bfloat16 [2, 8192, 14336], P('pipe', 'tp'), may hold values from -0.046875 to 0.046875
- adapter_reduce: bfloat16 [2, 128, 131072], P('pipe', None, 'tp'), may hold values from -0.0625 to 0.0625
- adapter_expand: bfloat16 [2, 128, 229376], P('pipe', None, 'tp'), may hold values from -1.5 to 1.5
Outputs:
- section_out: bfloat16 [2, 2, 120, 8192], P('pipe', 'rep', None, 'tp'), parts along dimension 1
There are 2 independent parts, one for each index of `rep`. A program takes and returns all parts, laid end to end along the dimension named above; an argument that names none is the same for every part. Nothing has to cross between parts.
Inputs may be any that keep to these rules, and one draw needn't show every extreme that they name: `segment_adapter`: within each micro-batch the adapter ids of its segments do not decrease. The first segment_requests[m, j] rows of segment j of micro-batch m hold requests; the other rows are padding.
All inputs are finite; a program needn't handle non-finite values.
Results may differ from a plain program's by a relative error of at most 0.0045.
Values may be sent and summed in bfloat16 or wider, within the bound.
No kernel may reach another device: no remote copies, remote signals or barrier semaphores. Data moves between devices by JAX's collectives and lax.ppermute only.
A program may use at most 128 MiB of HBM per device.

v0:
```python
import jax
import jax.numpy as jnp
from jax import lax
from jax.sharding import PartitionSpec as P

EPSILON = 1e-05


def shifted(x, axis, by):
    size = lax.axis_size(axis)
    pairs = [(i, i + by) for i in range(size) if 0 <= i + by < size]
    return lax.ppermute(x, axis, pairs)


def times_rows(left, weight):
    return lax.dot_general(
        left, weight, (((1,), (1,)), ((), ())), preferred_element_type=jnp.float32
    )


def block_step(
    current, unit_ids, unit_live, gain_full, up_weight, down_weight, shrink_weight, expand_weight
):
    row_count = current.shape[0]
    col_count = current.shape[1]
    hid_count = up_weight.shape[0]
    segments = unit_ids.shape[0]
    seg_rows = row_count // segments
    feature_width = gain_full.shape[0]
    adapter_rank_count = shrink_weight.shape[1] // col_count
    column = lax.axis_index("tp") * col_count
    gain_mine = lax.dynamic_slice_in_dim(gain_full, column, col_count, 0)
    widened_local = current.astype(jnp.float32)
    local_scaled = (widened_local * gain_mine).astype(jnp.bfloat16)
    input_panel = shrink_weight[unit_ids].reshape(segments, col_count, adapter_rank_count)
    output_panel = expand_weight[unit_ids].reshape(segments, hid_count, adapter_rank_count)
    partial_value = jnp.einsum(
        "sdr,spd->rsp",
        input_panel,
        local_scaled.reshape(segments, seg_rows, col_count),
        preferred_element_type=jnp.float32,
    ).reshape(adapter_rank_count, row_count)
    local_squares = jnp.sum(widened_local * widened_local, axis=1)
    reduced, squares = lax.psum((partial_value, local_squares), "tp")
    widened = lax.all_gather(current, "tp", axis=1, tiled=True).astype(jnp.float32)
    scaled = (widened * gain_full).astype(jnp.bfloat16)
    up_total = times_rows(scaled, up_weight)
    inverse = lax.rsqrt(squares / feature_width + EPSILON)
    low_rank = (
        (reduced * inverse[None, :])
        .astype(jnp.bfloat16)
        .reshape(adapter_rank_count, segments, seg_rows)
    )
    adapted = jnp.einsum(
        "rsp,sdr->spd", low_rank, output_panel, preferred_element_type=jnp.float32
    ).reshape(row_count, hid_count)
    up_sum = inverse[:, None] * up_total + adapted
    hidden_act = jax.nn.silu(up_sum).astype(jnp.bfloat16)
    down_sum = times_rows(lax.all_gather(hidden_act, "tp", axis=1, tiled=True), down_weight)
    updated = (widened_local + down_sum).astype(jnp.bfloat16)
    positions = lax.broadcasted_iota(jnp.int32, (segments, seg_rows), 1)
    row_kept = (positions < unit_live[:, None]).reshape(row_count, 1)
    return jnp.where(row_kept, updated, jnp.zeros_like(updated))


def run_window(
    units, unit_ids, unit_live, gain_full, up_weight, down_weight, shrink_weight, expand_weight
):
    section_index = lax.axis_index("pipe")
    sections = lax.axis_size("pipe")
    unit_count = units.shape[0]
    tick_total = unit_count + sections - 1

    def process(tick_index, received, collected):
        position = jnp.clip(tick_index - section_index, 0, unit_count - 1)
        arriving = lax.dynamic_index_in_dim(
            units, jnp.minimum(tick_index, unit_count - 1), 0, keepdims=False
        )
        current = jnp.where(section_index == 0, arriving, received)
        ids_here = lax.dynamic_index_in_dim(unit_ids, position, 0, keepdims=False)
        live_here = lax.dynamic_index_in_dim(unit_live, position, 0, keepdims=False)
        produced = block_step(
            current,
            ids_here,
            live_here,
            gain_full,
            up_weight,
            down_weight,
            shrink_weight,
            expand_weight,
        )
        lag = tick_index - section_index
        in_window = jnp.logical_and(lag >= 0, lag < unit_count)
        placed = lax.dynamic_update_index_in_dim(collected, produced, position, 0)
        return (produced, jnp.where(in_window, placed, collected))

    def one_tick(tick_index, state):
        produced, collected = process(tick_index, state[0], state[1])
        return (shifted(produced, "pipe", 1), collected)

    start_state = (jnp.zeros_like(units[0]), jnp.zeros_like(units))
    received, collected = lax.fori_loop(0, tick_total - 1, one_tick, start_state)
    produced, collected = process(tick_total - 1, received, collected)
    return collected


def per_device(
    hidden_entering,
    segment_adapter,
    segment_requests,
    section_norm_gain,
    up_matrix,
    down_matrix,
    adapter_reduce,
    adapter_expand,
):
    batch_list = hidden_entering.shape[0]
    row_count = hidden_entering.shape[1]
    col_count = hidden_entering.shape[2]
    collected = run_window(
        hidden_entering,
        segment_adapter,
        segment_requests,
        section_norm_gain[0],
        up_matrix[0],
        down_matrix[0],
        adapter_reduce[0],
        adapter_expand[0],
    )
    return collected.reshape(1, batch_list, row_count, col_count)


def solution(mesh):
    return jax.shard_map(
        per_device,
        mesh=mesh,
        in_specs=(
            P("rep", None, "tp"),
            P("rep", None),
            P("rep", None),
            P("pipe", None),
            P("pipe", "tp", None),
            P("pipe", "tp", None),
            P("pipe", None, "tp"),
            P("pipe", None, "tp"),
        ),
        out_specs=P("pipe", "rep", None, "tp"),
        check_vma=False,
    )
```

profile of v0, /device:TPU:0, one launch (start us, length us, event | category | flops | bytes accessed | tf_op | source)
XLA Modules:
  0.0 303.5 jit_solution(11378490578715964258)
XLA Ops:
  6.5 1.8 fusion.50
  8.4 0.7 fusion.60
  9.1 3.5 %gather_fusion = bf16[3,16384]{1,0:T(4,128)(2,1)S(1)} fusion(bf16[128,16384]{1,0:T(8,128)(2,1)} %bitcast.75, s32[1024]{0:T(1024)S(1)} %pad_clamp_fusion), kind=kCustom, calls=%fused_computation | custom fusion | bytes 196620 | tf_op jit(solution)/shard_map/while/body/eval_jaxpr/gather | solution.py:35
  12.6 0.6 reshape.115
  13.2 0.7 constant_dynamic-slice_fusion
  13.9 1.0 broadcast_select_fusion
  14.8 0.4 convolution_bitcast_fusion.1
  15.2 0.1 reshape.116
  15.3 23.9 %all-reduce.1 = (f32[16,120]{1,0:T(8,128)S(1)}, f32[120]{0:T(128)S(1)}) all-reduce(f32[16,120]{1,0:T(8,128)S(1)} %reshape.116, f32[120]{0:T(128)S(1)} %get-tuple-element.37), channel_id=1, replica_groups=mesh['rep'=2,'pipe'=2,'tp'=8] {'tp'}, use_global_device_ids=true, to_apply=%region_2.3 | all-reduce | flops 2040 | bytes 16320 | tf_op jit(solution)/shard_map/while/body/eval_jaxpr/psum | solution.py:44
  39.3 0.1 reshape.117
  39.4 4.9 %gather_fusion.1 = bf16[3,28672]{1,0:T(4,128)(2,1)S(1)} fusion(bf16[128,28672]{1,0:T(8,128)(2,1)} %bitcast.74, s32[1024]{0:T(1024)S(1)} %pad_clamp_fusion), kind=kCustom, calls=%fused_computation.1 | custom fusion | bytes 344076 | tf_op jit(solution)/shard_map/while/body/eval_jaxpr/gather | solution.py:36
  44.3 1.0 reshape.118
  45.3 0.6 fusion.58
  45.9 14.6 %all-gather.5.cloned.1.call-done = bf16[120,8192]{1,0:T(8,128)(2,1)} async-done(((bf16[120,1024]{1,0:T(8,128)(2,1)}), bf16[120,8192]{1,0:T(8,128)(2,1)}) %all-gather.5.cloned.1.call-update) | async-done | bytes 1966096 | tf_op jit(solution)/shard_map/while/body/eval_jaxpr/all_gather | solution.py:45
  60.5 15.4 %multiply_convert_fusion.7 = bf16[120,1792]{1,0:T(8,128)(2,1)} fusion(f32[120,1792]{1,0:T(8,128)S(1)} %bitcast.73, bf16[1,1792,8192]{2,1,0:T(8,128)(2,1)} %param.12, bf16[120,8192]{1,0:T(8,128)(2,1)} %all-gather.5.cloned.1.call-done, f32[8192]{0:T(1024)S(1)} %bitcast.78, f32[120]{0:T(128)S(1)} %add_rsqrt_fusion.1), kind=kOutput, calls=%fused_computation.29 | convolution fusion | flops 3527669760 | bytes 32649696 | tf_op jit(solution)/shard_map/while/body/eval_jaxpr/dot_general | solution.py:16
  76.0 0.1 iota_compare_fusion
  76.1 0.1 lt.71
  76.2 62.1 %all-gather.7.cloned.1.call-done = bf16[120,14336]{1,0:T(8,128)(2,1)} async-done(((bf16[120,1792]{1,0:T(8,128)(2,1)}), bf16[120,14336]{1,0:T(8,128)(2,1)}) %all-gather.7.cloned.1.call-update) | async-done | bytes 3440656 | tf_op jit(solution)/shard_map/while/body/eval_jaxpr/all_gather | solution.py:59
  138.3 14.8 %fusion.34 = bf16[120,1024]{1,0:T(8,128)(2,1)S(1)} fusion(bf16[120,14336]{1,0:T(8,128)(2,1)} %all-gather.7.cloned.1.call-done, bf16[1,1024,14336]{2,1,0:T(8,128)(2,1)} %param.13, bf16[120,1024]{1,0:T(8,128)(2,1)S(1)} %copy-done.1, pred[120]{0:T(512)(128)(4,1)S(1)} %lt.71), kind=kOutput, calls=%fused_computation.24 | convolution fusion | flops 3523706880 | bytes 33292408 | tf_op jit(solution)/shard_map/while/body/eval_jaxpr/dot_general | solution.py:16
  153.1 1.3 collective-permute-start
  154.4 1.1 collective-permute-done
  155.5 0.9 fusion.51
  156.4 1.0 fusion.52
  157.4 0.4 convolution_bitcast_fusion
  157.8 0.1 reshape.121
  157.9 20.4 %all-reduce = (f32[16,120]{1,0:T(8,128)S(1)}, f32[120]{0:T(128)S(1)}) all-reduce(f32[16,120]{1,0:T(8,128)S(1)} %reshape.121, f32[120]{0:T(128)S(1)} %get-tuple-element.35), channel_id=1, replica_groups=mesh['rep'=2,'pipe'=2,'tp'=8] {'tp'}, use_global_device_ids=true, to_apply=%region_5.6 | all-reduce | flops 2040 | bytes 16320 | tf_op jit(solution)/shard_map/psum | solution.py:44
  178.3 0.1 reshape.122
  178.4 0.6 fusion.56
  179.0 24.8 %all-gather.9.cloned.1.call-done = bf16[120,8192]{1,0:T(8,128)(2,1)} async-done(((bf16[120,1024]{1,0:T(8,128)(2,1)}), bf16[120,8192]{1,0:T(8,128)(2,1)}) %all-gather.9.cloned.1.call-update) | async-done | bytes 1966096 | tf_op jit(solution)/shard_map/all_gather | solution.py:45
  203.8 15.4 %multiply_convert_fusion.4 = bf16[120,1792]{1,0:T(8,128)(2,1)} fusion(f32[120,1792]{1,0:T(8,128)S(1)} %bitcast.72, bf16[1,1792,8192]{2,1,0:T(8,128)(2,1)} %param.12, bf16[120,8192]{1,0:T(8,128)(2,1)} %all-gather.9.cloned.1.call-done, f32[8192]{0:T(1024)S(1)} %bitcast.79, f32[120]{0:T(128)S(1)} %add_rsqrt_fusion), kind=kOutput, calls=%fused_computation.28 | convolution fusion | flops 3527669760 | bytes 32649696 | tf_op jit(solution)/shard_map/dot_general | solution.py:16
  219.2 62.3 %all-gather.11.cloned.1.call-done = bf16[120,14336]{1,0:T(8,128)(2,1)} async-done(((bf16[120,1792]{1,0:T(8,128)(2,1)}), bf16[120,14336]{1,0:T(8,128)(2,1)}) %all-gather.11.cloned.1.call-update) | async-done | bytes 3440656 | tf_op jit(solution)/shard_map/all_gather | solution.py:59
  281.5 15.5 %fusion.43 = bf16[1,1,120,1024]{3,2,1,0:T(8,128)(2,1)} fusion(bf16[120,14336]{1,0:T(8,128)(2,1)} %all-gather.11.cloned.1.call-done, bf16[1,1024,14336]{2,1,0:T(8,128)(2,1)} %param.13, bf16[120,1024]{1,0:T(8,128)(2,1)S(1)} %copy-done, bf16[120,1024]{1,0:T(8,128)(2,1)S(1)} %fusion.34, pred[120]{0:T(512)(128)(4,1)S(1)} %lt.71, pred[]{:T(512)S(6)} %and.10, ...), kind=kOutput, calls=%fused_computation.27 | convolution fusion | flops 3523952640 | bytes 33538170 | tf_op jit(solution)/shard_map/dot_general | solution.py:16
  (25 shorter events, 0.3 us)
Async XLA Ops:
  6.5 54.0 %all-gather.5.cloned.1.call-start = ((), (), s32[]{:S(2)}) async-start(), calls=%async_computation | async-start | bytes 2211840 | tf_op jit(solution)/shard_map/while/body/eval_jaxpr/all_gather | solution.py:45
  8.4 129.9 %all-gather.7.cloned.1.call-start = ((), (), s32[]{:S(2)}) async-start(), calls=%async_computation.1 | async-start | bytes 3870720 | tf_op jit(solution)/shard_map/while/body/eval_jaxpr/all_gather | solution.py:59
  14.8 45.7 %copy-start.3 = (f32[1,8192]{1,0:T(1,128)S(1)}, f32[1,8192]{1,0:T(1,128)}, u32[]{:S(2)}) copy-start(f32[1,8192]{1,0:T(1,128)} %param.11) | copy-start | bytes 98308
  60.5 15.5 %copy-start.4 = (s32[1,3]{1,0:T(1,128)S(1)}, s32[1,3]{1,0:T(1,128)}, u32[]{:S(2)}) copy-start(s32[1,3]{1,0:T(1,128)} %param.10) | copy-start | bytes 40
  60.5 77.7 %copy-start.1 = (bf16[120,1024]{1,0:T(8,128)(2,1)S(1)}, bf16[120,1024]{1,0:T(8,128)(2,1)}, u32[]{:S(2)}) copy-start(bf16[120,1024]{1,0:T(8,128)(2,1)} %get-tuple-element.38) | copy-start | bytes 737284
  76.0 127.8 %all-gather.9.cloned.1.call-start = ((), (), s32[]{:S(2)}) async-start(), calls=%async_computation.2 | async-start | bytes 2211840 | tf_op jit(solution)/shard_map/all_gather | solution.py:45
  76.2 79.3 %copy-start.2 = (bf16[1,120,1024]{2,1,0:T(8,128)(2,1)S(1)}, bf16[1,120,1024]{2,1,0:T(8,128)(2,1)}, u32[]{:S(2)}) copy-start(bf16[1,120,1024]{2,1,0:T(8,128)(2,1)} %param.8) | copy-start | bytes 737284
  153.1 2.4 collective-permute-start
  156.4 125.1 %all-gather.11.cloned.1.call-start = ((), (), s32[]{:S(2)}) async-start(), calls=%async_computation.3 | async-start | bytes 3870720 | tf_op jit(solution)/shard_map/all_gather | solution.py:59
  203.8 77.7 %copy-start = (bf16[120,1024]{1,0:T(8,128)(2,1)S(1)}, bf16[120,1024]{1,0:T(8,128)(2,1)}, u32[]{:S(2)}) copy-start(bf16[120,1024]{1,0:T(8,128)(2,1)} %get-tuple-element.36) | copy-start | bytes 737284
Sparse Core Ops, SparseCore 0:
  9.5 50.9 all-gather.4
  76.1 62.1 all-gather.6
  156.5 47.2 all-gather.8
  219.3 62.1 all-gather.10
where the time goes:
time: 304 us
  waiting for transfers between devices  165 us (54%)
  matrix products  63 us (21%)
  blocking collectives  44.3 us (15%)
  between operations  13.3 us (4%)
  local copies, waits for them, and re-layouts  11.2 us (4%)
  other arithmetic  5.41 us (2%)
    all_gather x2, waiting for transfers between devices, block_step(): lax.all_gather(hidden_act, 'tp', axis=1, tiled=True)  124 us
    dot_general x4, matrix products, times_rows(): lax.dot_general(left, weight, (((1,), (1,)), ((), ())), preferred_element...  61.1 us
    psum x2, blocking collectives, block_step(): reduced, squares = lax.psum((partial_value, local_squares), 'tp')  44.3 us
    all_gather x2, waiting for transfers between devices, block_step(): lax.all_gather(current, 'tp', axis=1, tiled=True).astype(jnp.float32)  39.3 us
  transfers between devices with their start and end apart: 5, of which 5 were waited for; matrix products, arithmetic and copies ran while one was open for 5% of the time, Pallas kernels for 0%

commit v1 on v0

--- a/solution.py
+++ b/solution.py
@@ -1,9 +1,17 @@
+import functools
+
 import jax
 import jax.numpy as jnp
 from jax import lax
+from jax.experimental import pallas as pl
+from jax.experimental.pallas import tpu as pltpu
 from jax.sharding import PartitionSpec as P
 
+
 EPSILON = 1e-05
+LANES = 128
+PIECES = 4
+VMEM_GRANT = 14 * 1024 * 1024
 
 
 def shifted(x, axis, by):
@@ -100,8 +108,472 @@
 
     start_state = (jnp.zeros_like(units[0]), jnp.zeros_like(units))
     received, collected = lax.fori_loop(0, tick_total - 1, one_tick, start_state)
-    produced, collected = process(tick_total - 1, received, collected)
+    _, collected = process(tick_total - 1, received, collected)
     return collected
+
+
+def vmem():
+    return pl.BlockSpec(memory_space=pltpu.VMEM)
+
+
+def smem():
+    return pl.BlockSpec(memory_space=pltpu.SMEM)
+
+
+def anywhere():
+    return pl.BlockSpec(memory_space=pltpu.MemorySpace.HBM)
+
+
+def in_hbm(x):
+    return pltpu.with_memory_space_constraint(x, pltpu.MemorySpace.HBM)
+
+
+def kernel_call(body, outs, flops, moved, name, aliases=None, scratch=()):
+    return dict(
+        kernel=body,
+        out_shape=outs,
+        input_output_aliases=aliases or {},
+        scratch_shapes=list(scratch),
+        compiler_params=pltpu.CompilerParams(vmem_limit_bytes=VMEM_GRANT),
+        cost_estimate=pl.CostEstimate(flops=flops, bytes_accessed=moved, transcendentals=0),
+        name=name,
+    )
+
+
+def fetch_body(info_ref, gain_ref, *refs, segments, id_at, own_at, cols, tables):
+    table_refs = refs[:tables]
+    outs = refs[tables : tables + tables * segments + 1]
+    buffers = refs[tables + tables * segments + 1 : -1]
+    sems = refs[-1]
+    copies = []
+    for t in range(tables):
+        for s in range(segments):
+            first = pl.multiple_of(info_ref[id_at + s] // 8 * 8, 8)
+            copies.append(
+                pltpu.make_async_copy(
+                    table_refs[t].at[pl.ds(first, 8), :],
+                    buffers[t].at[s],
+                    sems.at[t * segments + s],
+                )
+            )
+    for copy in copies:
+        copy.start()
+    start = pl.multiple_of(info_ref[own_at] * cols, cols)
+    outs[-1][...] = gain_ref[:, pl.ds(start, cols)]
+    for t in range(tables):
+        for s in range(segments):
+            copies[t * segments + s].wait()
+            block = buffers[t][s].astype(jnp.float32)
+            row = lax.broadcasted_iota(jnp.int32, block.shape, 0)
+            mine = jnp.where(row == info_ref[id_at + s] % 8, block, 0.0)
+            outs[t * segments + s][...] = jnp.sum(mine, axis=0, keepdims=True).astype(
+                jnp.bfloat16
+            )
+
+
+def fetch_rows(info, gain, tables, segments, id_at, own_at, cols):
+    outs = [
+        jax.ShapeDtypeStruct((1, t.shape[1]), jnp.bfloat16) for t in tables for _ in range(segments)
+    ] + [jax.ShapeDtypeStruct((1, cols), jnp.float32)]
+    spec = kernel_call(
+        functools.partial(
+            fetch_body,
+            segments=segments,
+            id_at=id_at,
+            own_at=own_at,
+            cols=cols,
+            tables=len(tables),
+        ),
+        tuple(outs),
+        0,
+        sum(16 * segments * t.shape[1] for t in tables),
+        "fetch",
+        scratch=[pltpu.VMEM((segments, 8, t.shape[1]), jnp.bfloat16) for t in tables]
+        + [pltpu.SemaphoreType.DMA((len(tables) * segments,))],
+    )
+    got = pl.pallas_call(
+        in_specs=[smem(), vmem()] + [anywhere()] * len(tables),
+        out_specs=(vmem(),) * len(outs),
+        **spec,
+    )(info, gain, *[in_hbm(t) for t in tables])
+    rows = [got[t * segments : (t + 1) * segments] for t in range(len(tables))]
+    return rows, got[-1]
+
+
+def write_payload(out_ref, rows, panel, seg_rows, rank):
+    row_count, cols = rows.shape
+    width = panel.shape[0]
+    both = lax.dot_general(
+        rows, panel, (((1,), (1,)), ((), ())), preferred_element_type=jnp.float32
+    )
+    owner = lax.broadcasted_iota(jnp.int32, (row_count, rank), 0)
+    part = jnp.zeros((row_count, rank), jnp.float32)
+    for s in range(width // rank):
+        inside = jnp.logical_and(owner >= s * seg_rows, owner < (s + 1) * seg_rows)
+        part = part + jnp.where(inside, both[:, s * rank : (s + 1) * rank], 0.0)
+    high = part.astype(jnp.bfloat16)
+    low = (part - high.astype(jnp.float32)).astype(jnp.bfloat16)
+    out_ref[:, :cols] = rows
+    out_ref[:, cols:] = jnp.concatenate(
+        [high, low, jnp.zeros((row_count, LANES - 2 * rank), jnp.bfloat16)], axis=1
+    )
+
+
+def payload_body(x_ref, panel_ref, out_ref, *, seg_rows, rank):
+    write_payload(out_ref, x_ref[...], panel_ref[...], seg_rows, rank)
+
+
+def make_payload(x, panel, seg_rows, rank):
+    rows, cols = x.shape
+    out = jax.ShapeDtypeStruct((rows, cols + LANES), jnp.bfloat16)
+    spec = kernel_call(
+        functools.partial(payload_body, seg_rows=seg_rows, rank=rank),
+        out,
+        2 * rows * cols * panel.shape[0],
+        4 * rows * cols,
+        "payload",
+    )
+    return pl.pallas_call(in_specs=[vmem(), vmem()], out_specs=vmem(), **spec)(x, panel)
+
+
+def chunk_copies(weight, targets, starts, depth, sems, base):
+    rows = weight.shape[0]
+    pieces = PIECES if rows % (PIECES * 16) == 0 else 1
+    size = rows // pieces
+    out = []
+    for c, (target, start) in enumerate(zip(targets, starts)):
+        for p in range(pieces):
+            part = pl.ds(p * size, size)
+            out.append(
+                pltpu.make_async_copy(
+                    weight.at[part, pl.ds(start, depth)],
+                    target.at[part, :],
+                    sems.at[(base + c) * PIECES + p],
+                )
+            )
+    return out
+
+
+def tile_of(size):
+    for parts in (2, 1):
+        if size % (parts * LANES) == 0:
+            return size // parts
+    return size
+
+
+def stage_body(info_ref, *refs, kind, gate, slots, later, begin, finish, shape):
+    row_count, depth, seg_rows, rank, features, segments, slot_at, live_at = shape
+    count = len(slots)
+    chunks, refs = refs[:count], refs[count:]
+    weight_ref, refs = refs[0], refs[1:]
+    if begin:
+        held = None
+    else:
+        held, refs = refs[:count], refs[count:]
+    if kind == "up":
+        gain_ref, refs = refs[0], refs[1:]
+    if finish == "act":
+        panel_ref, refs = refs[0], refs[1:]
+    if finish in ("next", "last"):
+        own_ref, side_ref, refs = refs[0], refs[1], refs[2:]
+    if not begin:
+        total_in, refs = refs[0], refs[1:]
+        if kind == "up":
+            stat_in, refs = refs[0], refs[1:]
+    ahead, refs = refs[: len(later)], refs[len(later) :]
+    if finish:
+        out_ref, refs = refs[0], refs[1:]
+        total_ref, stat_ref = None, None
+        if kind == "up":
+            stat_ref, refs = refs[0], refs[1:]
+    else:
+        total_ref, refs = refs[0], refs[1:]
+        if kind == "up":
+            stat_ref, refs = refs[0], refs[1:]
+    if begin:
+        held, refs = refs[:count], refs[count:]
+    sems = refs[0] if refs else None
+    width = weight_ref.shape[0]
+    tile = tile_of(width)
+    active = info_ref[gate] == 1
+
+    def start_of(slot):
+        return pl.multiple_of(info_ref[slot_at + slot] * depth, LANES)
+
+    @pl.when(active)
+    def _():
+        mine = []
+        if begin:
+            mine = chunk_copies(weight_ref, held, [start_of(s) for s in slots], depth, sems, 0)
+            for copy in mine:
+                copy.start()
+        base = count if begin else 0
+        coming = chunk_copies(weight_ref, ahead, [start_of(s) for s in later], depth, sems, base)
+        for copy in coming:
+            copy.start()
+        lefts = []
+        for c in range(count):
+            if kind == "down":
+                lefts.append(chunks[c][...])
+                continue
+            wide = chunks[c][:, :depth].astype(jnp.float32)
+            lefts.append((wide * gain_ref[:, pl.ds(start_of(slots[c]), depth)]).astype(jnp.bfloat16))
+            squares = jnp.sum(wide * wide, axis=1, keepdims=True)
+            extra = chunks[c][:, depth:].astype(jnp.float32)
+            low = extra[:, :rank] + extra[:, rank : 2 * rank]
+            stat = jnp.concatenate(
+                [low, jnp.broadcast_to(squares, (row_count, LANES - rank))], axis=1
+            )
+            if c == 0 and begin:
+                stat_ref[...] = stat
+            elif c == 0:
+                stat_ref[...] = stat_in[...] + stat
+            else:
+                stat_ref[...] += stat
+        if finish == "act":
+            inverse = lax.rsqrt(stat_ref[:, rank : rank + 1] / features + EPSILON)
+            low = (inverse * stat_ref[:, :rank]).astype(jnp.bfloat16)
+            across = panel_ref.shape[0]
+            tiled = jnp.concatenate([low] * segments, axis=1).astype(jnp.float32)
+            row = lax.broadcasted_iota(jnp.int32, (row_count, across), 0)
+            col = lax.broadcasted_iota(jnp.int32, (row_count, across), 1)
+            keep = jnp.zeros((row_count, across), jnp.bool_)
+            for s in range(segments):
+                rows_in = jnp.logical_and(row >= s * seg_rows, row < (s + 1) * seg_rows)
+                cols_in = jnp.logical_and(col >= s * rank, col < (s + 1) * rank)
+                keep = jnp.logical_or(keep, jnp.logical_and(rows_in, cols_in))
+            spread_low = jnp.where(keep, tiled, 0.0).astype(jnp.bfloat16)
+        if finish in ("next", "last"):
+            row = lax.broadcasted_iota(jnp.int32, (row_count, 1), 0)
+            keep = jnp.zeros((row_count, 1), jnp.bool_)
+            for s in range(segments):
+                end = info_ref[live_at + s] + s * seg_rows
+                keep = jnp.logical_or(keep, jnp.logical_and(row >= s * seg_rows, row < end))
+        for copy in mine:
+            copy.wait()
+
+        def one_tile(j):
+            part = pl.ds(pl.multiple_of(j * tile, tile), tile)
+            value = None if begin else total_in[:, part]
+            for c in range(count):
+                term = lax.dot_general(
+                    lefts[c],
+                    held[c][part, :],
+                    (((1,), (1,)), ((), ())),
+                    preferred_element_type=jnp.float32,
+                )
+                value = term if value is None else value + term
+            if finish == "act":
+                adapted = jnp.dot(
+                    spread_low, panel_ref[:, part], preferred_element_type=jnp.float32
+                )
+                value = inverse * value + adapted
+                out_ref[:, part] = (value / (1.0 + jnp.exp(-value))).astype(jnp.bfloat16)
+            elif finish:
+                value = own_ref[:, part].astype(jnp.float32) + value
+                out_ref[:, part] = jnp.where(keep, value, 0.0).astype(jnp.bfloat16)
+            else:
+                total_ref[:, part] = value
+
+        pl.loop(0, width // tile)(one_tile)
+        if finish == "next":
+            write_payload(out_ref, out_ref[:, :width], side_ref[...], seg_rows, rank)
+        for copy in coming:
+            copy.wait()
+
+    if finish == "last":
+
+        @pl.when(jnp.logical_not(active))
+        def _():
+            out_ref[...] = side_ref[:, :width]
+
+
+def stage_call(
+    kind, info, gate, slots, later, chunks, weight, held, state, shape, name, gain=None, extras=(),
+    finish=None,
+):
+    row_count, depth = shape[0], shape[1]
+    width = weight.shape[0]
+    begin = state is None
+    operands = [info] + list(chunks) + [in_hbm(weight)]
+    specs = [smem()] + [vmem()] * len(chunks) + [anywhere()]
+    if not begin:
+        operands += list(held)
+    if kind == "up":
+        operands.append(gain)
+    operands += list(extras)
+    aliases = {}
+    outs = [jax.ShapeDtypeStruct((width, depth), jnp.bfloat16) for _ in later]
+    if finish == "act":
+        outs.append(jax.ShapeDtypeStruct((row_count, width), jnp.bfloat16))
+    elif finish == "next":
+        outs.append(jax.ShapeDtypeStruct((row_count, width + LANES), jnp.bfloat16))
+    elif finish == "last":
+        outs.append(jax.ShapeDtypeStruct((row_count, width), jnp.bfloat16))
+    else:
+        outs.append(jax.ShapeDtypeStruct((row_count, width), jnp.float32))
+    if kind == "up":
+        outs.append(jax.ShapeDtypeStruct((row_count, LANES), jnp.float32))
+    if not begin:
+        if not finish:
+            aliases[len(operands)] = len(later)
+        operands.append(state[0])
+        if kind == "up":
+            aliases[len(operands)] = len(later) + 1
+            operands.append(state[1])
+    specs += [vmem()] * (len(operands) - len(specs))
+    scratch = []
+    if begin:
+        scratch += [pltpu.VMEM((width, depth), jnp.bfloat16) for _ in slots]
+    moving = len(later) + (len(slots) if begin else 0)
+    if moving:
+        scratch.append(pltpu.SemaphoreType.DMA((moving * PIECES,)))
+    spec = kernel_call(
+        functools.partial(
+            stage_body,
+            kind=kind,
+            gate=gate,
+            slots=tuple(slots),
+            later=tuple(later),
+            begin=begin,
+            finish=finish,
+            shape=shape,
+        ),
+        tuple(outs),
+        2 * row_count * width * depth * len(slots),
+        2 * width * depth * (len(slots) + len(later)),
+        name,
+        aliases,
+        scratch,
+    )
+    got = pl.pallas_call(in_specs=specs, out_specs=(vmem(),) * len(outs), **spec)(*operands)
+    return list(got[: len(later)]), list(got[len(later) :])
+
+
+def plan_of(rungs):
+    order = sorted(range(1, rungs), key=lambda k: min(k, rungs - k))
+    names = ["own", "x0"] + [f"z{k}" for k in order] + [f"f{k}" for k in order]
+    if not order:
+        return order, names, [["x0"]]
+    groups = [[f"z{order[0]}", "x0"]]
+    for a, b in zip(order, order[1:]):
+        groups.append([f"f{a}", f"z{b}"])
+    groups.append([f"f{order[-1]}"])
+    return order, names, groups
+
+
+def run_ladder(
+    rows, ids, live, gain, up_weight, down_weight, shrink_weight, expand_weight, rails
+):
+    row_count, cols = rows.shape
+    segments = ids.shape[0]
+    seg_rows = row_count // segments
+    rank = shrink_weight.shape[1] // cols
+    units = up_weight.shape[0]
+    features = gain.shape[0]
+    me = lax.axis_index("tp")
+    stage = lax.axis_index("pipe")
+    size = lax.axis_size("tp")
+    rungs = size // rails
+    rung, rail = me // rails, me % rails
+    order, names, groups = plan_of(rungs)
+
+    def send(value, source, target, move):
+        pairs = []
+        for t in range(size):
+            g, r = move(t // rails, t % rails)
+            pairs.append((source * size + t, target * size + g % rungs * rails + r))
+        return lax.ppermute(value, ("pipe", "tp"), pairs)
+
+    def owner(step, on):
+        return (rung - step + rungs) % rungs * rails + on
+
+    owners = {"own": me, "x0": owner(0, 1 - rail)}
+    for k in order:
+        owners[f"z{k}"] = owner(k, rail)
+        owners[f"f{k}"] = owner(k, 1 - rail)
+    gates = [(stage == k).astype(jnp.int32) for k in range(2)]
+    table = jnp.stack(gates + [owners[n].astype(jnp.int32) for n in names])
+    info = jnp.concatenate([table, live, ids])
+    slot_at, live_at = 2, 2 + len(names)
+    id_at = live_at + segments
+    slot = {n: i for i, n in enumerate(names)}
+
+    gain_row = gain.reshape(1, features)
+    (shrink_rows,), gain_mine = fetch_rows(
+        info, gain_row, [shrink_weight], segments, id_at, slot_at, cols
+    )
+    reduce_panel = jnp.concatenate(
+        [r.reshape(1, cols, rank).transpose(0, 2, 1) for r in shrink_rows]
+    )
+    reduce_panel = (
+        (reduce_panel.astype(jnp.float32) * gain_mine[:, None, :])
+        .astype(jnp.bfloat16)
+        .reshape(segments * rank, cols)
+    )
+    swap = [(i, (i + size) % (2 * size)) for i in range(2 * size)]
+    partner_panel = lax.ppermute(reduce_panel, ("pipe", "tp"), swap)
+    first_panel = jnp.where(stage == 0, reduce_panel, partner_panel)
+    carried = make_payload(rows, first_panel, seg_rows, rank)
+    (expand_rows,), _ = fetch_rows(
+        info, gain_row, [expand_weight], segments, id_at, slot_at, cols
+    )
+    expand_panel = jnp.concatenate(
+        [r.reshape(1, units, rank).transpose(0, 2, 1) for r in expand_rows]
+    ).reshape(segments * rank, units)
+
+    def gather(value, worker):
+        helper = 1 - worker
+        got = {}
+        for k in order:
+            got[f"z{k}"] = send(value, helper, worker, lambda g, r, k=k: (g + k, r))
+        got["x0"] = send(value, helper, worker, lambda g, r: (g, 1 - r))
+        for k in order:
+            got[f"f{k}"] = send(got[f"z{k}"], worker, worker, lambda g, r: (g, 1 - r))
+        return got
+
+    def multiply(kind, own, got, weight, gate, depth, phase, gain=None, extras=(), finish=None):
+        shape = (row_count, depth, seg_rows, rank, features, segments, slot_at, live_at)
+        held, state = None, None
+        steps = [["own"]] + groups
+        for i, group in enumerate(steps):
+            later = [slot[n] for n in steps[i + 1]] if i + 1 < len(steps) else []
+            last = not later
+            held, state = stage_call(
+                kind,
+                info,
+                gate,
+                [slot[n] for n in group],
+                later,
+                [own if n == "own" else got[n] for n in group],
+                weight,
+                held,
+                state,
+                shape,
+                phase + ("_own" if i == 0 else f"_{i - 1}"),
+                gain=gain,
+                extras=extras if last else (),
+                finish=finish if last else None,
+            )
+        return state[0]
+
+    for k in range(2):
+        worker, helper = k, 1 - k
+        own = carried
+        if k:
+            own = send(carried, helper, worker, lambda g, r: (g, r))
+        got = gather(carried, worker)
+        act = multiply(
+            "up", own, got, up_weight, k, cols, f"{k}x", gain_row, (expand_panel,), "act"
+        )
+        handed = send(act, worker, helper, lambda g, r: (g, r))
+        got = gather(handed, worker)
+        side = partner_panel if k == 0 else carried
+        carried = multiply(
+            "down", act, got, down_weight, k, units, f"{k}a", None, (own, side),
+            "next" if k == 0 else "last",
+        )
+    return carried
 
 
 def per_device(
@@ -117,6 +589,29 @@
     batch_list = hidden_entering.shape[0]
     row_count = hidden_entering.shape[1]
     col_count = hidden_entering.shape[2]
+    size = lax.axis_size("tp")
+    rails = 2
+    fits = (
+        lax.axis_size("pipe") == 2
+        and batch_list == 1
+        and size % rails == 0
+        and size // rails <= 4
+        and col_count % LANES == 0
+        and up_matrix.shape[1] % LANES == 0
+    )
+    if fits:
+        out = run_ladder(
+            hidden_entering[0],
+            segment_adapter[0],
+            segment_requests[0],
+            section_norm_gain[0],
+            up_matrix[0],
+            down_matrix[0],
+            adapter_reduce[0],
+            adapter_expand[0],
+            rails,
+        )
+        return out.reshape(1, batch_list, row_count, col_count)
     collected = run_window(
         hidden_entering,
         segment_adapter,

time: 304 us -> 182 us (0.60)
  the two profiles are of different devices: /device:TPU:0 before, /device:TPU:1 now
where the time goes in v1:
time: 182 us; the launch traced here: 181 us
  waiting for transfers between devices  75.1 us (41%)
  starting transfers between devices  51.4 us (28%)
  Pallas kernels  48.4 us (27%)
  local copies, waits for them, and re-layouts  3.94 us (2%)
    ppermute x31, waiting for transfers between devices, send(): return lax.ppermute(value, ('pipe', 'tp'), pairs)  73.8 us
    ppermute x31, starting transfers between devices, send(): return lax.ppermute(value, ('pipe', 'tp'), pairs)  51.3 us
    pallas_call x20, Pallas kernels, stage_call(): pl.pallas_call(in_specs=specs, out_specs=(vmem(),) * len(outs), **spec)  43.2 us
    pallas_call x2, Pallas kernels, fetch_rows(): pl.pallas_call(in_specs=[smem(), vmem()] + [anywhere()] * len(tables), ou...  4.86 us
  transfers between devices with their start and end apart: 32, of which 10 were waited for; matrix products, arithmetic and copies ran while one was open for 1% of the time, Pallas kernels for 22%

profile of v1, /device:TPU:1, one launch (start us, length us, event | category | flops | bytes accessed | tf_op | source)
XLA Modules:
  0.0 181.2 jit_solution(2920648603235377882)
XLA Ops:
  1.5 2.1 %fetch.2 = (bf16[1,16384]{1,0:T(2,128)(2,1)S(1)}, bf16[1,16384]{1,0:T(2,128)(2,1)S(1)}, bf16[1,16384]{1,0:T(2,128)(2,1)S(1)}, f32[1,1024]{1,0:T(1,128)S(1)}) custom-call(s32[16]{0:T(128)S(1)} %concatenate.9.info_ref, f32[1,8192]{1,0:T(1,128)S(1)} %copy-done, bf16[128,16384]{1,0:T(8,128)(2,1)} %bitcast.57), custom_call_target="tpu_custom_call" | custom-call | bytes 786432 | tf_op jit(solution)/shard_map/fetch/pallas_call | solution.py:194
  6.9 4.6 %collective-permute-start.5 = (bf16[120,1152]{1,0:T(8,128)(2,1)S(1)}, bf16[120,1152]{1,0:T(8,128)(2,1)S(1)}, u32[]{:S(2)}, u32[]{:S(2)}) collective-permute-start(bf16[120,1152]{1,0:T(8,128)(2,1)S(1)} %payload.1.refs_0_.refs_3_), channel_id=1, source_target_pairs={{8,2},{9,3},{10,4},{11,5},{12,6},{13,7},{14,0},{15,1},{24,18},{25,... | collective-permute-start | bytes 829448 | tf_op jit(solution)/shard_map/ppermute | solution.py:486
  11.5 3.3 %collective-permute-start.3 = (bf16[120,1152]{1,0:T(8,128)(2,1)S(1)}, bf16[120,1152]{1,0:T(8,128)(2,1)S(1)}, u32[]{:S(2)}, u32[]{:S(2)}) collective-permute-start(bf16[120,1152]{1,0:T(8,128)(2,1)S(1)} %payload.1.refs_0_.refs_3_), channel_id=1, source_target_pairs={{8,6},{9,7},{10,0},{11,1},{12,2},{13,3},{14,4},{15,5},{24,22},{25,... | collective-permute-start | bytes 829448 | tf_op jit(solution)/shard_map/ppermute | solution.py:486
  17.5 2.8 %fetch.3 = (bf16[1,28672]{1,0:T(2,128)(2,1)S(1)}, bf16[1,28672]{1,0:T(2,128)(2,1)S(1)}, bf16[1,28672]{1,0:T(2,128)(2,1)S(1)}, f32[1,1024]{1,0:T(1,128)}) custom-call(s32[16]{0:T(128)S(1)} %concatenate.9.info_ref, f32[1,8192]{1,0:T(1,128)S(1)} %copy-done.1, bf16[128,28672]{1,0:T(8,128)(2,1)} %bitcast.56), custom_call_target="tpu_custom_call" | custom-call | bytes 1376256 | tf_op jit(solution)/shard_map/fetch/pallas_call | solution.py:194
  29.4 22.3 %collective-permute-done.8 = bf16[120,1792]{1,0:T(8,128)(2,1)S(1)} collective-permute-done((bf16[120,1792]{1,0:T(8,128)(2,1)S(1)}, bf16[120,1792]{1,0:T(8,128)(2,1)S(1)}, u32[]{:S(2)}, u32[]{:S(2)}) %collective-permute-start.8) | collective-permute-done | bytes 430112 | tf_op jit(solution)/shard_map/ppermute | solution.py:486
  53.0 3.6 %collective-permute-start.11 = (bf16[120,1792]{1,0:T(8,128)(2,1)S(1)}, bf16[120,1792]{1,0:T(8,128)(2,1)S(1)}, u32[]{:S(2)}, u32[]{:S(2)}) collective-permute-start(bf16[120,1792]{1,0:T(8,128)(2,1)S(1)} %collective-permute-done.8), channel_id=1, source_target_pairs={{8,6},{9,7},{10,0},{11,1},{12,2},{13,3},{14,4},{15,5},{24,22},{25,... | collective-permute-start | bytes 1290248 | tf_op jit(solution)/shard_map/ppermute | solution.py:486
  56.6 1.3 collective-permute-start.9
  57.9 1.3 collective-permute-start.15
  59.9 2.8 %collective-permute-done.11.refs_1_ = bf16[120,1792]{1,0:T(8,128)(2,1)S(1)} collective-permute-done((bf16[120,1792]{1,0:T(8,128)(2,1)S(1)}, bf16[120,1792]{1,0:T(8,128)(2,1)S(1)}, u32[]{:S(2)}, u32[]{:S(2)}) %collective-permute-start.11) | collective-permute-done | bytes 430112 | tf_op jit(solution)/shard_map/ppermute | solution.py:486
  63.4 3.9 %collective-permute-done.9.refs_1_ = bf16[120,1792]{1,0:T(8,128)(2,1)S(1)} collective-permute-done((bf16[120,1792]{1,0:T(8,128)(2,1)S(1)}, bf16[120,1792]{1,0:T(8,128)(2,1)S(1)}, u32[]{:S(2)}, u32[]{:S(2)}) %collective-permute-start.9) | collective-permute-done | bytes 430112 | tf_op jit(solution)/shard_map/ppermute | solution.py:486
  77.8 24.4 %collective-permute-done.20.refs_0_ = bf16[120,1152]{1,0:T(8,128)(2,1)S(1)} collective-permute-done((bf16[120,1152]{1,0:T(8,128)(2,1)S(1)}, bf16[120,1152]{1,0:T(8,128)(2,1)S(1)}, u32[]{:S(2)}, u32[]{:S(2)}) %collective-permute-start.20) | collective-permute-done | bytes 276512 | tf_op jit(solution)/shard_map/ppermute | solution.py:486
  102.2 3.1 %collective-permute-start.21 = (bf16[120,1152]{1,0:T(8,128)(2,1)S(1)}, bf16[120,1152]{1,0:T(8,128)(2,1)S(1)}, u32[]{:S(2)}, u32[]{:S(2)}) collective-permute-start(bf16[120,1152]{1,0:T(8,128)(2,1)S(1)} %collective-permute-done.20.refs_0_), channel_id=1, source_target_pairs={{8,9},{9,8},{10,11},{11,10},{12,13},{13,12},{14,15},{15,14},{24,25... | collective-permute-start | bytes 829448 | tf_op jit(solution)/shard_map/ppermute | solution.py:486
  105.3 2.2 %collective-permute-start.19 = (bf16[120,1152]{1,0:T(8,128)(2,1)S(1)}, bf16[120,1152]{1,0:T(8,128)(2,1)S(1)}, u32[]{:S(2)}, u32[]{:S(2)}) collective-permute-start(bf16[120,1152]{1,0:T(8,128)(2,1)S(1)} %collective-permute-done.18.refs_1_), channel_id=1, source_target_pairs={{8,9},{9,8},{10,11},{11,10},{12,13},{13,12},{14,15},{15,14},{24,25... | collective-permute-start | bytes 829448 | tf_op jit(solution)/shard_map/ppermute | solution.py:486
  107.5 3.5 %collective-permute-done.16.refs_1_ = bf16[120,1152]{1,0:T(8,128)(2,1)S(1)} collective-permute-done((bf16[120,1152]{1,0:T(8,128)(2,1)S(1)}, bf16[120,1152]{1,0:T(8,128)(2,1)S(1)}, u32[]{:S(2)}, u32[]{:S(2)}) %collective-permute-start.16) | collective-permute-done | bytes 276512 | tf_op jit(solution)/shard_map/ppermute | solution.py:486
  111.0 3.1 %collective-permute-start.17 = (bf16[120,1152]{1,0:T(8,128)(2,1)S(1)}, bf16[120,1152]{1,0:T(8,128)(2,1)S(1)}, u32[]{:S(2)}, u32[]{:S(2)}) collective-permute-start(bf16[120,1152]{1,0:T(8,128)(2,1)S(1)} %collective-permute-done.16.refs_1_), channel_id=1, source_target_pairs={{8,9},{9,8},{10,11},{11,10},{12,13},{13,12},{14,15},{15,14},{24,25... | collective-permute-start | bytes 829448 | tf_op jit(solution)/shard_map/ppermute | solution.py:486
  114.1 4.9 %_x_own.3 = (bf16[1792,1024]{1,0:T(8,128)(2,1)S(1)}, bf16[1792,1024]{1,0:T(8,128)(2,1)S(1)}, f32[120,1792]{1,0:T(8,128)S(1)}, f32[120,128]{1,0:T(8,128)S(1)}) custom-call(s32[16]{0:T(128)S(1)} %concatenate.9.info_ref, bf16[120,1152]{1,0:T(8,128)(2,1)S(1)} %collective-permute-done.23.refs_0_.refs_3_, bf16[1792,8192]{1,0:T(8,128)(2,1)} %bitcast.41, ...), custom_call_target="tpu_custom_call" | custom-call | flops 440401920 | bytes 11010048 | tf_op jit(solution)/shard_map/1x_own/pallas_call | solution.py:449
  119.1 3.9 %_x_0.3 = (bf16[1792,1024]{1,0:T(8,128)(2,1)S(1)}, bf16[1792,1024]{1,0:T(8,128)(2,1)S(1)}, f32[120,1792]{1,0:T(8,128)S(1)}, f32[120,128]{1,0:T(8,128)S(1)}) custom-call(s32[16]{0:T(128)S(1)} %concatenate.9.info_ref, bf16[120,1152]{1,0:T(8,128)(2,1)S(1)} %collective-permute-done.20.refs_0_, ...), custom_call_target="tpu_custom_call", output_to_operand_aliasing={{2}: (7, {}), {3}: (8, {})} | custom-call | flops 880803840 | bytes 14680064 | tf_op jit(solution)/shard_map/1x_0/pallas_call | solution.py:449
  123.0 3.9 %_x_1.3 = (bf16[1792,1024]{1,0:T(8,128)(2,1)S(1)}, bf16[1792,1024]{1,0:T(8,128)(2,1)S(1)}, f32[120,1792]{1,0:T(8,128)S(1)}, f32[120,128]{1,0:T(8,128)S(1)}) custom-call(s32[16]{0:T(128)S(1)} %concatenate.9.info_ref, bf16[120,1152]{1,0:T(8,128)(2,1)S(1)} %collective-permute-done.21.refs_0_, ...), custom_call_target="tpu_custom_call", output_to_operand_aliasing={{2}: (7, {}), {3}: (8, {})} | custom-call | flops 880803840 | bytes 14680064 | tf_op jit(solution)/shard_map/1x_1/pallas_call | solution.py:449
  126.9 3.4 %_x_2.3 = (bf16[1792,1024]{1,0:T(8,128)(2,1)S(1)}, f32[120,1792]{1,0:T(8,128)S(1)}, f32[120,128]{1,0:T(8,128)S(1)}) custom-call(s32[16]{0:T(128)S(1)} %concatenate.9.info_ref, bf16[120,1152]{1,0:T(8,128)(2,1)S(1)} %collective-permute-done.19.refs_0_, ...), custom_call_target="tpu_custom_call", output_to_operand_aliasing={{1}: (7, {}), {2}: (8, {})} | custom-call | flops 880803840 | bytes 11010048 | tf_op jit(solution)/shard_map/1x_2/pallas_call | solution.py:449
  130.3 2.5 %_x_3.3 = (bf16[120,1792]{1,0:T(8,128)(2,1)S(1)}, f32[120,128]{1,0:T(8,128)S(1)}) custom-call(s32[16]{0:T(128)S(1)} %concatenate.9.info_ref, bf16[120,1152]{1,0:T(8,128)(2,1)S(1)} %collective-permute-done.17.refs_0_, bf16[1792,8192]{1,0:T(8,128)(2,1)} %bitcast.45, ...), custom_call_target="tpu_custom_call", output_to_operand_aliasing={{1}: (7, {})} | custom-call | flops 440401920 | bytes 3670016 | tf_op jit(solution)/shard_map/1x_3/pallas_call | solution.py:449
  134.2 1.4 collective-permute-done.24
  140.7 6.2 %collective-permute-done.29.refs_0_ = bf16[120,1792]{1,0:T(8,128)(2,1)S(1)} collective-permute-done((bf16[120,1792]{1,0:T(8,128)(2,1)S(1)}, bf16[120,1792]{1,0:T(8,128)(2,1)S(1)}, u32[]{:S(2)}, u32[]{:S(2)}) %collective-permute-start.29) | collective-permute-done | bytes 430112 | tf_op jit(solution)/shard_map/ppermute | solution.py:486
  146.9 2.2 %collective-permute-start.30 = (bf16[120,1792]{1,0:T(8,128)(2,1)S(1)}, bf16[120,1792]{1,0:T(8,128)(2,1)S(1)}, u32[]{:S(2)}, u32[]{:S(2)}) collective-permute-start(bf16[120,1792]{1,0:T(8,128)(2,1)S(1)} %collective-permute-done.29.refs_0_), channel_id=1, source_target_pairs={{8,9},{9,8},{10,11},{11,10},{12,13},{13,12},{14,15},{15,14},{24,25... | collective-permute-start | bytes 1290248 | tf_op jit(solution)/shard_map/ppermute | solution.py:486
  149.1 1.8 collective-permute-done.27.refs_1_
  150.9 2.2 %collective-permute-start.28 = (bf16[120,1792]{1,0:T(8,128)(2,1)S(1)}, bf16[120,1792]{1,0:T(8,128)(2,1)S(1)}, u32[]{:S(2)}, u32[]{:S(2)}) collective-permute-start(bf16[120,1792]{1,0:T(8,128)(2,1)S(1)} %collective-permute-done.27.refs_1_), channel_id=1, source_target_pairs={{8,9},{9,8},{10,11},{11,10},{12,13},{13,12},{14,15},{15,14},{24,25... | collective-permute-start | bytes 1290248 | tf_op jit(solution)/shard_map/ppermute | solution.py:486
  153.1 7.5 %collective-permute-done.25.refs_1_ = bf16[120,1792]{1,0:T(8,128)(2,1)S(1)} collective-permute-done((bf16[120,1792]{1,0:T(8,128)(2,1)S(1)}, bf16[120,1792]{1,0:T(8,128)(2,1)S(1)}, u32[]{:S(2)}, u32[]{:S(2)}) %collective-permute-start.25) | collective-permute-done | bytes 430112 | tf_op jit(solution)/shard_map/ppermute | solution.py:486
  160.6 2.2 %collective-permute-start.26 = (bf16[120,1792]{1,0:T(8,128)(2,1)S(1)}, bf16[120,1792]{1,0:T(8,128)(2,1)S(1)}, u32[]{:S(2)}, u32[]{:S(2)}) collective-permute-start(bf16[120,1792]{1,0:T(8,128)(2,1)S(1)} %collective-permute-done.25.refs_1_), channel_id=1, source_target_pairs={{8,9},{9,8},{10,11},{11,10},{12,13},{13,12},{14,15},{15,14},{24,25... | collective-permute-start | bytes 1290248 | tf_op jit(solution)/shard_map/ppermute | solution.py:486
  162.9 4.8 %_a_own.3 = (bf16[1024,1792]{1,0:T(8,128)(2,1)S(1)}, bf16[1024,1792]{1,0:T(8,128)(2,1)S(1)}, f32[120,1024]{1,0:T(8,128)S(1)}) custom-call(s32[16]{0:T(128)S(1)} %concatenate.9.info_ref, bf16[120,1792]{1,0:T(8,128)(2,1)S(1)} %get-tuple-element.115.refs_0_, bf16[1024,14336]{1,0:T(8,128)(2,1)} %bitcast.51), custom_call_target="tpu_custom_call" | custom-call | flops 440401920 | bytes 11010048 | tf_op jit(solution)/shard_map/1a_own/pallas_call | solution.py:449
  167.7 3.7 %_a_0.3 = (bf16[1024,1792]{1,0:T(8,128)(2,1)S(1)}, bf16[1024,1792]{1,0:T(8,128)(2,1)S(1)}, f32[120,1024]{1,0:T(8,128)S(1)}) custom-call(s32[16]{0:T(128)S(1)} %concatenate.9.info_ref, bf16[120,1792]{1,0:T(8,128)(2,1)S(1)} %collective-permute-done.29.refs_0_, bf16[120,1792]{1,0:T(8,128)(2,1)S(1)} %collective-permute-done.31.refs_1_, ...), custom_call_target="tpu_custom_call", output_to_operand_aliasing={{2}: (6, {})} | custom-call | flops 880803840 | bytes 14680064 | tf_op jit(solution)/shard_map/1a_0/pallas_call | solution.py:449
  171.5 3.7 %_a_1.3 = (bf16[1024,1792]{1,0:T(8,128)(2,1)S(1)}, bf16[1024,1792]{1,0:T(8,128)(2,1)S(1)}, f32[120,1024]{1,0:T(8,128)S(1)}) custom-call(s32[16]{0:T(128)S(1)} %concatenate.9.info_ref, bf16[120,1792]{1,0:T(8,128)(2,1)S(1)} %collective-permute-done.30.refs_0_, bf16[120,1792]{1,0:T(8,128)(2,1)S(1)} %collective-permute-done.27.refs_1_, ...), custom_call_target="tpu_custom_call", output_to_operand_aliasing={{2}: (6, {})} | custom-call | flops 880803840 | bytes 14680064 | tf_op jit(solution)/shard_map/1a_1/pallas_call | solution.py:449
  175.2 3.2 %_a_2.3 = (bf16[1024,1792]{1,0:T(8,128)(2,1)S(1)}, f32[120,1024]{1,0:T(8,128)S(1)}) custom-call(s32[16]{0:T(128)S(1)} %concatenate.9.info_ref, bf16[120,1792]{1,0:T(8,128)(2,1)S(1)} %collective-permute-done.28.refs_0_, bf16[120,1792]{1,0:T(8,128)(2,1)S(1)} %collective-permute-done.25.refs_1_, ...), custom_call_target="tpu_custom_call", output_to_operand_aliasing={{1}: (6, {})} | custom-call | flops 880803840 | bytes 11010048 | tf_op jit(solution)/shard_map/1a_2/pallas_call | solution.py:449
  178.5 2.8 %_a_3.3 = bf16[120,1024]{1,0:T(8,128)(2,1)} custom-call(s32[16]{0:T(128)S(1)} %concatenate.9.info_ref, bf16[120,1792]{1,0:T(8,128)(2,1)S(1)} %collective-permute-done.26.refs_0_, bf16[1024,14336]{1,0:T(8,128)(2,1)} %bitcast.55, bf16[1024,1792]{1,0:T(8,128)(2,1)S(1)} %get-tuple-element.125.refs_2_, ...), custom_call_target="tpu_custom_call" | custom-call | flops 440401920 | bytes 3670016 | tf_op jit(solution)/shard_map/1a_3/pallas_call | solution.py:449
  (84 shorter events, 35.9 us)
Async XLA Ops:
  5.2 1.4 collective-permute-start
  6.9 15.9 %collective-permute-start.5 = (bf16[120,1152]{1,0:T(8,128)(2,1)S(1)}, bf16[120,1152]{1,0:T(8,128)(2,1)S(1)}, u32[]{:S(2)}, u32[]{:S(2)}) collective-permute-start(bf16[120,1152]{1,0:T(8,128)(2,1)S(1)} %payload.1.refs_0_.refs_3_), channel_id=1, source_target_pairs={{8,2},{9,3},{10,4},{11,5},{12,6},{13,7},{14,0},{15,1},{24,18},{25,... | collective-permute-start | bytes 829448 | tf_op jit(solution)/shard_map/ppermute | solution.py:486
  11.5 12.0 %collective-permute-start.3 = (bf16[120,1152]{1,0:T(8,128)(2,1)S(1)}, bf16[120,1152]{1,0:T(8,128)(2,1)S(1)}, u32[]{:S(2)}, u32[]{:S(2)}) collective-permute-start(bf16[120,1152]{1,0:T(8,128)(2,1)S(1)} %payload.1.refs_0_.refs_3_), channel_id=1, source_target_pairs={{8,6},{9,7},{10,0},{11,1},{12,2},{13,3},{14,4},{15,5},{24,22},{25,... | collective-permute-start | bytes 829448 | tf_op jit(solution)/shard_map/ppermute | solution.py:486
  14.9 9.4 %collective-permute-start.1 = (bf16[120,1152]{1,0:T(8,128)(2,1)S(1)}, bf16[120,1152]{1,0:T(8,128)(2,1)S(1)}, u32[]{:S(2)}, u32[]{:S(2)}) collective-permute-start(bf16[120,1152]{1,0:T(8,128)(2,1)S(1)} %payload.1.refs_0_.refs_3_), channel_id=1, source_target_pairs={{8,4},{9,5},{10,6},{11,7},{12,0},{13,1},{14,2},{15,3},{24,20},{25,... | collective-permute-start | bytes 829448 | tf_op jit(solution)/shard_map/ppermute | solution.py:486
  16.2 9.4 %collective-permute-start.7 = (bf16[120,1152]{1,0:T(8,128)(2,1)S(1)}, bf16[120,1152]{1,0:T(8,128)(2,1)S(1)}, u32[]{:S(2)}, u32[]{:S(2)}) collective-permute-start(bf16[120,1152]{1,0:T(8,128)(2,1)S(1)} %payload.1.refs_0_.refs_3_), channel_id=1, source_target_pairs={{8,1},{9,0},{10,3},{11,2},{12,5},{13,4},{14,7},{15,6},{24,17},{25,... | collective-permute-start | bytes 829448 | tf_op jit(solution)/shard_map/ppermute | solution.py:486
  22.8 3.4 %collective-permute-start.6 = (bf16[120,1152]{1,0:T(8,128)(2,1)S(1)}, bf16[120,1152]{1,0:T(8,128)(2,1)S(1)}, u32[]{:S(2)}, u32[]{:S(2)}) collective-permute-start(bf16[120,1152]{1,0:T(8,128)(2,1)S(1)} %collective-permute-done.5.refs_0_), channel_id=1, source_target_pairs={{0,1},{1,0},{2,3},{3,2},{4,5},{5,4},{6,7},{7,6},{16,17},{17,16},{1... | collective-permute-start | bytes 829448 | tf_op jit(solution)/shard_map/ppermute | solution.py:486
  23.5 3.4 %collective-permute-start.4 = (bf16[120,1152]{1,0:T(8,128)(2,1)S(1)}, bf16[120,1152]{1,0:T(8,128)(2,1)S(1)}, u32[]{:S(2)}, u32[]{:S(2)}) collective-permute-start(bf16[120,1152]{1,0:T(8,128)(2,1)S(1)} %collective-permute-done.3.refs_1_), channel_id=1, source_target_pairs={{0,1},{1,0},{2,3},{3,2},{4,5},{5,4},{6,7},{7,6},{16,17},{17,16},{1... | collective-permute-start | bytes 829448 | tf_op jit(solution)/shard_map/ppermute | solution.py:486
  24.3 3.2 %collective-permute-start.2 = (bf16[120,1152]{1,0:T(8,128)(2,1)S(1)}, bf16[120,1152]{1,0:T(8,128)(2,1)S(1)}, u32[]{:S(2)}, u32[]{:S(2)}) collective-permute-start(bf16[120,1152]{1,0:T(8,128)(2,1)S(1)} %collective-permute-done.1.refs_1_), channel_id=1, source_target_pairs={{0,1},{1,0},{2,3},{3,2},{4,5},{5,4},{6,7},{7,6},{16,17},{17,16},{1... | collective-permute-start | bytes 829448 | tf_op jit(solution)/shard_map/ppermute | solution.py:486
  28.1 23.6 %collective-permute-start.8 = (bf16[120,1792]{1,0:T(8,128)(2,1)S(1)}, bf16[120,1792]{1,0:T(8,128)(2,1)S(1)}, u32[]{:S(2)}, u32[]{:S(2)}) collective-permute-start(bf16[120,1792]{1,0:T(8,128)(2,1)S(1)} %get-tuple-element.88.refs_0_), channel_id=1, source_target_pairs={{0,8},{1,9},{2,10},{3,11},{4,12},{5,13},{6,14},{7,15},{16,24},{17,... | collective-permute-start | bytes 1290248 | tf_op jit(solution)/shard_map/ppermute | solution.py:486
  51.6 7.6 %collective-permute-start.13 = (bf16[120,1792]{1,0:T(8,128)(2,1)S(1)}, bf16[120,1792]{1,0:T(8,128)(2,1)S(1)}, u32[]{:S(2)}, u32[]{:S(2)}) collective-permute-start(bf16[120,1792]{1,0:T(8,128)(2,1)S(1)} %collective-permute-done.8), channel_id=1, source_target_pairs={{8,2},{9,3},{10,4},{11,5},{12,6},{13,7},{14,0},{15,1},{24,18},{25,... | collective-permute-start | bytes 1290248 | tf_op jit(solution)/shard_map/ppermute | solution.py:486
  53.0 9.8 %collective-permute-start.11 = (bf16[120,1792]{1,0:T(8,128)(2,1)S(1)}, bf16[120,1792]{1,0:T(8,128)(2,1)S(1)}, u32[]{:S(2)}, u32[]{:S(2)}) collective-permute-start(bf16[120,1792]{1,0:T(8,128)(2,1)S(1)} %collective-permute-done.8), channel_id=1, source_target_pairs={{8,6},{9,7},{10,0},{11,1},{12,2},{13,3},{14,4},{15,5},{24,22},{25,... | collective-permute-start | bytes 1290248 | tf_op jit(solution)/shard_map/ppermute | solution.py:486
  56.6 10.8 %collective-permute-start.9 = (bf16[120,1792]{1,0:T(8,128)(2,1)S(1)}, bf16[120,1792]{1,0:T(8,128)(2,1)S(1)}, u32[]{:S(2)}, u32[]{:S(2)}) collective-permute-start(bf16[120,1792]{1,0:T(8,128)(2,1)S(1)} %collective-permute-done.8), channel_id=1, source_target_pairs={{8,4},{9,5},{10,6},{11,7},{12,0},{13,1},{14,2},{15,3},{24,20},{25,... | collective-permute-start | bytes 1290248 | tf_op jit(solution)/shard_map/ppermute | solution.py:486
  57.9 10.8 %collective-permute-start.15 = (bf16[120,1792]{1,0:T(8,128)(2,1)S(1)}, bf16[120,1792]{1,0:T(8,128)(2,1)S(1)}, u32[]{:S(2)}, u32[]{:S(2)}) collective-permute-start(bf16[120,1792]{1,0:T(8,128)(2,1)S(1)} %collective-permute-done.8), channel_id=1, source_target_pairs={{8,1},{9,0},{10,3},{11,2},{12,5},{13,4},{14,7},{15,6},{24,17},{25,... | collective-permute-start | bytes 1290248 | tf_op jit(solution)/shard_map/ppermute | solution.py:486
  59.2 10.3 %collective-permute-start.14 = (bf16[120,1792]{1,0:T(8,128)(2,1)S(1)}, bf16[120,1792]{1,0:T(8,128)(2,1)S(1)}, u32[]{:S(2)}, u32[]{:S(2)}) collective-permute-start(bf16[120,1792]{1,0:T(8,128)(2,1)S(1)} %collective-permute-done.13.refs_0_), channel_id=1, source_target_pairs={{0,1},{1,0},{2,3},{3,2},{4,5},{5,4},{6,7},{7,6},{16,17},{17,16},{1... | collective-permute-start | bytes 1290248 | tf_op jit(solution)/shard_map/ppermute | solution.py:486
  62.7 7.4 %collective-permute-start.12 = (bf16[120,1792]{1,0:T(8,128)(2,1)S(1)}, bf16[120,1792]{1,0:T(8,128)(2,1)S(1)}, u32[]{:S(2)}, u32[]{:S(2)}) collective-permute-start(bf16[120,1792]{1,0:T(8,128)(2,1)S(1)} %collective-permute-done.11.refs_1_), channel_id=1, source_target_pairs={{0,1},{1,0},{2,3},{3,2},{4,5},{5,4},{6,7},{7,6},{16,17},{17,16},{1... | collective-permute-start | bytes 1290248 | tf_op jit(solution)/shard_map/ppermute | solution.py:486
  67.3 3.4 %collective-permute-start.10 = (bf16[120,1792]{1,0:T(8,128)(2,1)S(1)}, bf16[120,1792]{1,0:T(8,128)(2,1)S(1)}, u32[]{:S(2)}, u32[]{:S(2)}) collective-permute-start(bf16[120,1792]{1,0:T(8,128)(2,1)S(1)} %collective-permute-done.9.refs_1_), channel_id=1, source_target_pairs={{0,1},{1,0},{2,3},{3,2},{4,5},{5,4},{6,7},{7,6},{16,17},{17,16},{1... | collective-permute-start | bytes 1290248 | tf_op jit(solution)/shard_map/ppermute | solution.py:486
  71.3 30.9 %collective-permute-start.20 = (bf16[120,1152]{1,0:T(8,128)(2,1)S(1)}, bf16[120,1152]{1,0:T(8,128)(2,1)S(1)}, u32[]{:S(2)}, u32[]{:S(2)}) collective-permute-start(bf16[120,1152]{1,0:T(8,128)(2,1)S(1)} %_a_3.2.refs_4_), channel_id=1, source_target_pairs={{0,10},{1,11},{2,12},{3,13},{4,14},{5,15},{6,8},{7,9},{16,26},{17,... | collective-permute-start | bytes 829448 | tf_op jit(solution)/shard_map/ppermute | solution.py:486
  72.6 32.7 %collective-permute-start.18 = (bf16[120,1152]{1,0:T(8,128)(2,1)S(1)}, bf16[120,1152]{1,0:T(8,128)(2,1)S(1)}, u32[]{:S(2)}, u32[]{:S(2)}) collective-permute-start(bf16[120,1152]{1,0:T(8,128)(2,1)S(1)} %_a_3.2.refs_4_), channel_id=1, source_target_pairs={{0,14},{1,15},{2,8},{3,9},{4,10},{5,11},{6,12},{7,13},{16,30},{17,... | collective-permute-start | bytes 829448 | tf_op jit(solution)/shard_map/ppermute | solution.py:486
  73.9 37.1 %collective-permute-start.16 = (bf16[120,1152]{1,0:T(8,128)(2,1)S(1)}, bf16[120,1152]{1,0:T(8,128)(2,1)S(1)}, u32[]{:S(2)}, u32[]{:S(2)}) collective-permute-start(bf16[120,1152]{1,0:T(8,128)(2,1)S(1)} %_a_3.2.refs_4_), channel_id=1, source_target_pairs={{0,12},{1,13},{2,14},{3,15},{4,8},{5,9},{6,10},{7,11},{16,28},{17,... | collective-permute-start | bytes 829448 | tf_op jit(solution)/shard_map/ppermute | solution.py:486
  75.2 38.9 %collective-permute-start.23 = (bf16[120,1152]{1,0:T(8,128)(2,1)S(1)}, bf16[120,1152]{1,0:T(8,128)(2,1)S(1)}, u32[]{:S(2)}, u32[]{:S(2)}) collective-permute-start(bf16[120,1152]{1,0:T(8,128)(2,1)S(1)} %_a_3.2.refs_4_), channel_id=1, source_target_pairs={{0,8},{1,9},{2,10},{3,11},{4,12},{5,13},{6,14},{7,15},{16,24},{17,... | collective-permute-start | bytes 829448 | tf_op jit(solution)/shard_map/ppermute | solution.py:486
  76.5 42.5 %collective-permute-start.22 = (bf16[120,1152]{1,0:T(8,128)(2,1)S(1)}, bf16[120,1152]{1,0:T(8,128)(2,1)S(1)}, u32[]{:S(2)}, u32[]{:S(2)}) collective-permute-start(bf16[120,1152]{1,0:T(8,128)(2,1)S(1)} %_a_3.2.refs_4_), channel_id=1, source_target_pairs={{0,9},{1,8},{2,11},{3,10},{4,13},{5,12},{6,15},{7,14},{16,25},{17,... | collective-permute-start | bytes 829448 | tf_op jit(solution)/shard_map/ppermute | solution.py:486
  102.2 20.8 %collective-permute-start.21 = (bf16[120,1152]{1,0:T(8,128)(2,1)S(1)}, bf16[120,1152]{1,0:T(8,128)(2,1)S(1)}, u32[]{:S(2)}, u32[]{:S(2)}) collective-permute-start(bf16[120,1152]{1,0:T(8,128)(2,1)S(1)} %collective-permute-done.20.refs_0_), channel_id=1, source_target_pairs={{8,9},{9,8},{10,11},{11,10},{12,13},{13,12},{14,15},{15,14},{24,25... | collective-permute-start | bytes 829448 | tf_op jit(solution)/shard_map/ppermute | solution.py:486
  105.3 21.5 %collective-permute-start.19 = (bf16[120,1152]{1,0:T(8,128)(2,1)S(1)}, bf16[120,1152]{1,0:T(8,128)(2,1)S(1)}, u32[]{:S(2)}, u32[]{:S(2)}) collective-permute-start(bf16[120,1152]{1,0:T(8,128)(2,1)S(1)} %collective-permute-done.18.refs_1_), channel_id=1, source_target_pairs={{8,9},{9,8},{10,11},{11,10},{12,13},{13,12},{14,15},{15,14},{24,25... | collective-permute-start | bytes 829448 | tf_op jit(solution)/shard_map/ppermute | solution.py:486
  111.0 19.3 %collective-permute-start.17 = (bf16[120,1152]{1,0:T(8,128)(2,1)S(1)}, bf16[120,1152]{1,0:T(8,128)(2,1)S(1)}, u32[]{:S(2)}, u32[]{:S(2)}) collective-permute-start(bf16[120,1152]{1,0:T(8,128)(2,1)S(1)} %collective-permute-done.16.refs_1_), channel_id=1, source_target_pairs={{8,9},{9,8},{10,11},{11,10},{12,13},{13,12},{14,15},{15,14},{24,25... | collective-permute-start | bytes 829448 | tf_op jit(solution)/shard_map/ppermute | solution.py:486
  132.9 2.7 %collective-permute-start.24 = (bf16[120,1792]{1,0:T(8,128)(2,1)S(1)}, bf16[120,1792]{1,0:T(8,128)(2,1)S(1)}, u32[]{:S(2)}, u32[]{:S(2)}) collective-permute-start(bf16[120,1792]{1,0:T(8,128)(2,1)S(1)} %get-tuple-element.115.refs_0_), channel_id=1, source_target_pairs={{8,0},{9,1},{10,2},{11,3},{12,4},{13,5},{14,6},{15,7},{24,16},{25,... | collective-permute-start | bytes 1290248 | tf_op jit(solution)/shard_map/ppermute | solution.py:486
  135.5 11.4 %collective-permute-start.29 = (bf16[120,1792]{1,0:T(8,128)(2,1)S(1)}, bf16[120,1792]{1,0:T(8,128)(2,1)S(1)}, u32[]{:S(2)}, u32[]{:S(2)}) collective-permute-start(bf16[120,1792]{1,0:T(8,128)(2,1)S(1)} %collective-permute-done.24), channel_id=1, source_target_pairs={{0,10},{1,11},{2,12},{3,13},{4,14},{5,15},{6,8},{7,9},{16,26},{17,... | collective-permute-start | bytes 1290248 | tf_op jit(solution)/shard_map/ppermute | solution.py:486
  136.8 14.1 %collective-permute-start.27 = (bf16[120,1792]{1,0:T(8,128)(2,1)S(1)}, bf16[120,1792]{1,0:T(8,128)(2,1)S(1)}, u32[]{:S(2)}, u32[]{:S(2)}) collective-permute-start(bf16[120,1792]{1,0:T(8,128)(2,1)S(1)} %collective-permute-done.24), channel_id=1, source_target_pairs={{0,14},{1,15},{2,8},{3,9},{4,10},{5,11},{6,12},{7,13},{16,30},{17,... | collective-permute-start | bytes 1290248 | tf_op jit(solution)/shard_map/ppermute | solution.py:486
  138.1 22.5 %collective-permute-start.25 = (bf16[120,1792]{1,0:T(8,128)(2,1)S(1)}, bf16[120,1792]{1,0:T(8,128)(2,1)S(1)}, u32[]{:S(2)}, u32[]{:S(2)}) collective-permute-start(bf16[120,1792]{1,0:T(8,128)(2,1)S(1)} %collective-permute-done.24), channel_id=1, source_target_pairs={{0,12},{1,13},{2,14},{3,15},{4,8},{5,9},{6,10},{7,11},{16,28},{17,... | collective-permute-start | bytes 1290248 | tf_op jit(solution)/shard_map/ppermute | solution.py:486
  139.4 28.3 %collective-permute-start.31 = (bf16[120,1792]{1,0:T(8,128)(2,1)S(1)}, bf16[120,1792]{1,0:T(8,128)(2,1)S(1)}, u32[]{:S(2)}, u32[]{:S(2)}) collective-permute-start(bf16[120,1792]{1,0:T(8,128)(2,1)S(1)} %collective-permute-done.24), channel_id=1, source_target_pairs={{0,9},{1,8},{2,11},{3,10},{4,13},{5,12},{6,15},{7,14},{16,25},{17,... | collective-permute-start | bytes 1290248 | tf_op jit(solution)/shard_map/ppermute | solution.py:486
  146.9 24.5 %collective-permute-start.30 = (bf16[120,1792]{1,0:T(8,128)(2,1)S(1)}, bf16[120,1792]{1,0:T(8,128)(2,1)S(1)}, u32[]{:S(2)}, u32[]{:S(2)}) collective-permute-start(bf16[120,1792]{1,0:T(8,128)(2,1)S(1)} %collective-permute-done.29.refs_0_), channel_id=1, source_target_pairs={{8,9},{9,8},{10,11},{11,10},{12,13},{13,12},{14,15},{15,14},{24,25... | collective-permute-start | bytes 1290248 | tf_op jit(solution)/shard_map/ppermute | solution.py:486
  150.9 24.3 %collective-permute-start.28 = (bf16[120,1792]{1,0:T(8,128)(2,1)S(1)}, bf16[120,1792]{1,0:T(8,128)(2,1)S(1)}, u32[]{:S(2)}, u32[]{:S(2)}) collective-permute-start(bf16[120,1792]{1,0:T(8,128)(2,1)S(1)} %collective-permute-done.27.refs_1_), channel_id=1, source_target_pairs={{8,9},{9,8},{10,11},{11,10},{12,13},{13,12},{14,15},{15,14},{24,25... | collective-permute-start | bytes 1290248 | tf_op jit(solution)/shard_map/ppermute | solution.py:486
  160.6 17.8 %collective-permute-start.26 = (bf16[120,1792]{1,0:T(8,128)(2,1)S(1)}, bf16[120,1792]{1,0:T(8,128)(2,1)S(1)}, u32[]{:S(2)}, u32[]{:S(2)}) collective-permute-start(bf16[120,1792]{1,0:T(8,128)(2,1)S(1)} %collective-permute-done.25.refs_1_), channel_id=1, source_target_pairs={{8,9},{9,8},{10,11},{11,10},{12,13},{13,12},{14,15},{15,14},{24,25... | collective-permute-start | bytes 1290248 | tf_op jit(solution)/shard_map/ppermute | solution.py:486
  (3 other events, 21.8 us)
